TPU v7x, 256 devices: a whole 4x4x8 slice. The times are simulated.
256 devices in a mesh: depth: 8 (over z_hi, x), lat: 32 (over y, z_lo, core).
Axes of the slice: x: 4, y: 4, z: 8 (z_hi: 2, z_lo: 4; z = z_hi * 4 + z_lo), core: 2. Of those that a mesh axis runs over, the one named last changes fastest.
Arguments:
- displacement: float32 [3, 64, 256, 256], P(None, 'depth', 'lat'), may hold values from -6 to 6
- velocity: float32 [3, 64, 256, 256], P(None, 'depth', 'lat'), may hold values from -6 to 6
- inverse_mass: float32 [64, 256, 256], P('depth', 'lat'), may hold values from 0.5 to 2
- material: int32 [64, 256, 256], P('depth', 'lat'), may hold values from 0 to 7
- dilation_table: float32 [8], replicated, may hold values from 0.5 to 2
- shear_table: float32 [8], replicated, may hold values from 0.5 to 2
- stiffness_pair: float32 [2, 24, 24], replicated, may hold values from -1.5 to 3.5, as said below
- impedance: float32 [3], replicated, may hold values from 0.5 to 2
- bedrock_mask: int32 [256, 256], P('lat'), may hold values 0 or 1
- incident: float32 [6, 3, 256, 256], P(None, None, 'lat'), may hold values from -6 to 6
Outputs:
- new_displacement: float32 [3, 64, 256, 256], P(None, 'depth', 'lat')
- new_velocity: float32 [3, 64, 256, 256], P(None, 'depth', 'lat')
Inputs may be any that keep to these rules, and one draw needn't show every extreme that they name: `stiffness_pair`: symmetric positive definite.
All inputs are finite; a program needn't handle non-finite values. No bound on the sum of `bedrock_mask` on one device may be relied on, other than what follows from the above.
Results may differ from a plain program's by a relative error of at most 0.00016.
Values sent between devices are 32-bit elements; how exact they have to be, the bound alone decides.
A program may use at most 64 MiB of HBM per device.

v0:
```python
import functools

import jax
import jax.numpy as jnp
from jax import lax
from jax.experimental import pallas as pl
from jax.experimental.pallas import tpu as pltpu
from jax.sharding import PartitionSpec as P

MESH = pl.DeviceIdType.MESH
DT = 0.1
f32, bf16, i32 = jnp.float32, jnp.bfloat16, jnp.int32
DIRECTIONS = ((1, 0), (-1, 0), (1, 1), (1, -1), (-1, 1), (-1, -1), (0, 1), (0, -1))

KL = 80
KB = 2 * KL
KP = 512
MO = 384
MH = 512


def kernel(
    nd, nl,
    u_in, v_in, im_in, mat_in, dil_in, she_in, k_in, imp_in, mask_in, inc_in,
    u_out, v_out,
    W, HW, Q, HQ, BI, HB, MI, KV, MV, IV, E, WM, XH, XL, PR, FD, FH, HIM,
    dil, she, imp,
    in_sem, send_sem, recv_sem, qsend_sem, qrecv_sem, bsend_sem, brecv_sem,
):
    steps = inc_in.shape[0]
    rounds = steps // 2
    nz, ny, nx = im_in.shape
    d = lax.axis_index("depth")
    l = lax.axis_index("lat")

    def exists(dz, dy):
        return ((d + dz >= 0) & (d + dz < nd)) & ((l + dy >= 0) & (l + dy < nl))

    own = pl.ds(2, nz)
    loads = [(im_in, Q.at[own, 0]), (mat_in, MI)]
    for c in range(3):
        loads.append((u_in.at[c], W.at[0, own, 1, c]))
        loads.append((v_in.at[c], W.at[0, own, 0, c]))
    first = len(loads)
    loads += [(k_in, KV), (mask_in, MV), (inc_in, IV), (dil_in, dil), (she_in, she), (imp_in, imp)]
    loads = [pltpu.make_async_copy(a, b, in_sem.at[i]) for i, (a, b) in enumerate(loads)]
    for load in loads:
        load.start()

    barrier = pltpu.get_barrier_semaphore()
    partners = 0
    for dz, dy in DIRECTIONS:
        @pl.when(exists(dz, dy))
        def _():
            pl.semaphore_signal(barrier, inc=1, device_id=(d + dz, l + dy), device_id_type=MESH)
        partners = partners + exists(dz, dy).astype(i32)
    for load in loads[:first]:
        load.wait()
    for z in range(nz):
        Q[z + 2, 1] = MI[z].astype(f32)
    pl.semaphore_wait(barrier, partners)

    def remote(src, dst, ss, rs, dz, dy):
        return pltpu.make_async_remote_copy(
            src_ref=src, dst_ref=dst, send_sem=ss, recv_sem=rs,
            device_id=(d + dz, l + dy), device_id_type=MESH)

    def layers(dz):
        if dz == 0:
            return own, own
        return (pl.ds(nz, 2), pl.ds(0, 2)) if dz == 1 else (pl.ds(2, 2), pl.ds(nz + 2, 2))

    def copies(t, k):
        dz, dy = DIRECTIONS[k]
        a, b = layers(dz)
        if dy == 0:
            near, far = (nz + 1, nz) if dz == 1 else (2, 3)
            to_near, to_far = (1, 0) if dz == 1 else (nz + 2, nz + 3)
            pairs = [(W.at[t, near], W.at[t, to_near]), (W.at[t, far, 1], W.at[t, to_far, 1])]
        else:
            rows, to = ((ny - 1, ny - 2), pl.ds(0, 3)) if dy == 1 else ((0, 1), pl.ds(3, 3))
            pairs = [(W.at[t, a, :, :, rows[0]], HW.at[t, b, pl.ds(0, 2), to]),
                     (W.at[t, a, 1, :, rows[1]], HW.at[t, b, 2, to])]
        return [remote(src, dst, send_sem.at[t // 2, 2 * k + i], recv_sem.at[t // 2, 2 * k + i], dz, dy)
                for i, (src, dst) in enumerate(pairs)]

    def q_copies(k):
        dz, dy = DIRECTIONS[k]
        a, b = layers(dz)
        if dy == 0:
            pairs = [(Q.at[a], Q.at[b])]
        elif dy == 1:
            pairs = [(Q.at[a, :, ny - 1], HQ.at[b, :, 0]), (Q.at[a, :, ny - 2], HQ.at[b, :, 1])]
        else:
            pairs = [(Q.at[a, :, 0], HQ.at[b, :, 2])]
        return [remote(src, dst, qsend_sem.at[2 * k + i], qrecv_sem.at[2 * k + i], dz, dy)
                for i, (src, dst) in enumerate(pairs)]

    def b_copy(dy):
        row, to, i = (ny - 1, pl.ds(0, 3), 0) if dy == 1 else (0, pl.ds(3, 3), 1)
        return remote(BI.at[:, 0, :, row], HB.at[:, to], bsend_sem.at[i], brecv_sem.at[i], 0, dy)

    def for_all(make, backward, act):
        for k, (dz, dy) in enumerate(DIRECTIONS):
            sign = -1 if backward else 1

            @pl.when(exists(sign * dz, sign * dy))
            def _():
                for copy in make(k):
                    act(copy)

    def for_bottom(backward, act):
        for dy in (1, -1):
            @pl.when((d == nd - 1) & exists(0, -dy if backward else dy))
            def _():
                act(b_copy(dy))

    start = lambda copy: copy.start()
    for_all(lambda k: copies(0, k) + q_copies(k), False, start)

    for load in loads[first:]:
        load.wait()
    for r in range(rounds):
        for i in range(2):
            for c in range(3):
                BI[r, i, c] = 2.0 * MV[...].astype(f32) * IV[2 * r + i, c]
    for_bottom(False, start)

    def clear(n):
        for t in range(0, steps, 2):
            W[t, n] = jnp.zeros_like(W[t, n])
            HW[t, n] = jnp.zeros_like(HW[t, n])
        Q[n, 0] = jnp.zeros_like(Q[n, 0])
        Q[n, 1] = jnp.full_like(Q[n, 1], -1.0)
        HQ[n, 0] = jnp.zeros_like(HQ[n, 0])
        HQ[n, 1] = jnp.full_like(HQ[n, 1], -1.0)

    @pl.when(d == 0)
    def _():
        clear(0)
        clear(1)

    @pl.when(d == nd - 1)
    def _():
        clear(nz + 2)
        clear(nz + 3)

    def clear_side(rows, q_rows):
        for n in range(nz + 4):
            for t in range(0, steps, 2):
                for i in range(3):
                    HW[t, n, i, rows[0]:rows[1]] = jnp.zeros((3, nx), f32)
            HQ[n, 0, q_rows[0]:q_rows[1]] = jnp.zeros((q_rows[1] - q_rows[0], nx), f32)
            HQ[n, 1, q_rows[0]:q_rows[1]] = jnp.full((q_rows[1] - q_rows[0], nx), -1.0, f32)
        for r in range(rounds):
            HB[r, rows[0]:rows[1]] = jnp.zeros((3, nx), f32)

    @pl.when(l == 0)
    def _():
        clear_side((0, 3), (0, 2))

    @pl.when(l == nl - 1)
    def _():
        clear_side((3, 6), (2, 3))

    row = lax.broadcasted_iota(i32, (ny, nx), 0)
    lane = lax.broadcasted_iota(i32, (ny, nx), 1)

    def column_dofs(shape):
        j = lax.broadcasted_iota(i32, shape, 1)
        block = (j >= KB).astype(i32) + (j >= 2 * KB).astype(i32) + (j >= 3 * KB).astype(i32)
        j = j - KB * block
        bz = (j >= KL).astype(i32)
        j = j - KL * bz
        inner = j < 48
        bx_i = (j >= 24).astype(i32)
        c_i = (j - 24 * bx_i) >> 3
        y_i = j & 7
        h = j - 48
        far = (h >= 16).astype(i32)
        bx_h = (h >> 3) & 1
        r = h & 7
        s = (r >= 3).astype(i32)
        c_h = r - 3 * s
        y_h = jnp.where(r >= 6, 99, jnp.where(s == 0, -1 - far, 8 + far))
        y = jnp.where(inner, y_i, y_h)
        bx = jnp.where(inner, bx_i, bx_h)
        c = jnp.where(inner, c_i, c_h)
        return block, jnp.where(block < 3, y, 99), 12 * bz + 3 * bx + c

    block, _, dof = column_dofs((24, KP))
    i24 = lax.broadcasted_iota(i32, (24, KP), 0)
    stiff = jnp.concatenate([KV[0], KV[1]], 0)
    block48, _, _ = column_dofs((48, KP))
    for by in (0, 1):
        one_hot = (i24 == dof + 6 * by).astype(f32)
        e = jnp.dot(stiff, one_hot, precision=lax.Precision.HIGHEST, preferred_element_type=f32)
        e_hi = e.astype(bf16).astype(f32)
        E[by] = jnp.where(block48 == 2, e - e_hi, e_hi)
    _, y_col, _ = column_dofs((8, KP))
    r8 = lax.broadcasted_iota(i32, (8, KP), 0)
    y_halo = jnp.where(r8 < 3, -1, jnp.where(r8 < 6, 8, 199))

    def band(y_row, ay, picks):
        e0, e1 = picks
        delta = y_col - y_row + ay
        return jnp.where(delta == 0, e0, jnp.where(delta == 1, e1, 0.0))

    def wide(by, q):
        return jnp.broadcast_to(E[by, q:q + 1], (8, KP))

    for q in range(0, 48, 2):
        tiles = [band(r8, (p // 6) % 2, (wide(0, p), wide(1, p))) for p in (q, q + 1)]
        WM[8 * q:8 * q + 16] = jnp.concatenate(tiles, 0).astype(bf16)
    for g in range(0, 16, 2):
        tiles = []
        for p in (g, g + 1):
            picks = []
            for by in (0, 1):
                a, b, c = (wide(by, 3 * p + i) for i in range(3))
                picks.append(jnp.where((r8 == 0) | (r8 == 3), a, jnp.where((r8 == 1) | (r8 == 4), b, c)))
            tiles.append(band(y_halo, (p // 2) % 2, picks))
        WM[MO + 8 * g:MO + 8 * g + 16] = jnp.concatenate(tiles, 0).astype(bf16)

    def fields(n):
        def full(x):
            return jnp.broadcast_to(x, (ny, nx))
        mat = Q[n, 1]
        m1, m2, m8 = full(HQ[n, 1, 0:1]), full(HQ[n, 1, 1:2]), full(HQ[n, 1, 2:3])
        m7 = full(Q[n, 1, ny - 1:ny])
        before = jnp.where(row == 0, m1, pltpu.roll(mat, 1, 0))
        for ref, ay, m in ((FD, 0, mat), (FD, 1, before), (FH, 0, jnp.where(row < 3, m1, m8)),
                           (FH, 1, jnp.where(row < 3, m2, m7))):
            for f, table in ((0, dil), (1, she)):
                value = jnp.zeros((ny, nx), f32)
                for level in range(table.shape[0]):
                    value = jnp.where(m == float(level), table[level], value)
                ref[n, f, ay] = value

    def masses(n):
        low, high = HQ[n, 0, 0:1], HQ[n, 0, 2:3]
        HIM[n] = DT * jnp.where(row < 3, jnp.broadcast_to(low, (ny, nx)), jnp.broadcast_to(high, (ny, nx)))

    for_all(q_copies, True, lambda copy: copy.wait_recv())
    for_bottom(True, lambda copy: copy.wait_recv())

    @pl.loop(0, nz + 3)
    def _(n):
        fields(n)
        masses(n)

    at_bottom = (d == nd - 1).astype(f32)
    imp_rows = jnp.where((row == 0) | (row == 3), imp[0], jnp.where((row == 1) | (row == 4), imp[1], imp[2]))

    def ahead(x):
        return jnp.where(lane == nx - 1, 0.0, pltpu.roll(x, nx - 1, 1))

    def behind(x):
        return jnp.where(lane == 0, 0.0, pltpu.roll(x, 1, 1))

    def operand(t, n, extended):
        tiles = [W[t, n, 1, c] for c in range(3)]
        halo = [jnp.where(row < 6, HW[t, n, 1], 0.0)]
        if extended:
            halo.append(jnp.where(row < 6, HW[t, n, 2], 0.0))
        parts = tiles + [ahead(x) for x in tiles]
        for x in halo:
            parts += [x, ahead(x)]
        if not extended:
            parts += [jnp.zeros((ny, nx), f32)] * 2
        x = jnp.concatenate(parts, 0)
        hi = x.astype(bf16)
        XH[n] = hi
        XL[n] = (x - hi.astype(f32)).astype(bf16)

    def step(t, r, extended):
        first_e, last_e = (0, nz + 3) if extended else (1, nz + 2)
        m = MH if extended else MO
        for n in range(first_e, last_e + 1):
            operand(t, n, extended)
        carry = None
        for e in range(first_e, last_e):
            x = jnp.concatenate([XH[e], XH[e + 1], XL[e], XL[e + 1], XH[e], XH[e + 1],
                                 jnp.zeros((KP - 3 * KB, nx), bf16)], 0)
            slot = e % 2
            PR[slot, 0:m] = jnp.dot(WM[0:m], x, preferred_element_type=f32)

            def gather(az):
                sums = {}
                for ax in (0, 1):
                    for c in range(4 if extended else 3):
                        total = None
                        for f in (0, 1):
                            for ay in (0, 1):
                                g = 8 * f + 4 * az + 2 * ay + ax
                                if c < 3:
                                    at = 8 * (3 * g + c)
                                    term = FD[e, f, ay] * PR[slot, at:at + 8]
                                else:
                                    at = MO + 8 * g
                                    term = FH[e, f, ay] * PR[slot, at:at + 8]
                                total = term if total is None else total + term
                        sums[ax, c] = total
                return sums

            if carry is not None:
                sums = gather(0)
                force = [sums[0, c] + carry[0, c] + behind(sums[1, c] + carry[1, c])
                         for c in range(4 if extended else 3)]
                scale = DT * Q[e, 0]
                for c in range(3):
                    net = -force[c]
                    v = W[t, e, 0, c]
                    if e == nz + 1:
                        net = net + at_bottom * imp[c] * (BI[t // 2, r, c] - v)
                    v = v + scale * net
                    W[t + 1, e, 0, c] = v
                    W[t + 1, e, 1, c] = W[t, e, 1, c] + DT * v
                if extended:
                    net = -force[3]
                    v = HW[t, e, 0]
                    if e == nz + 1:
                        net = net + at_bottom * imp_rows * (HB[t // 2] - v)
                    v = v + HIM[e] * net
                    HW[t + 1, e, 1] = HW[t, e, 1] + DT * v
            carry = gather(1)

    @pl.loop(0, rounds)
    def _(i):
        t = 2 * i

        @pl.when(i > 0)
        def _():
            for_all(lambda k: copies(t, k), False, start)

        for_all(lambda k: copies(t, k), True, lambda copy: copy.wait_recv())
        step(t, 0, True)
        step(t + 1, 1, False)

    for z in range(nz):
        for c in range(3):
            u_out[c, z] = W[steps, z + 2, 1, c]
            v_out[c, z] = W[steps, z + 2, 0, c]

    done = lambda copy: copy.wait_send()
    for_all(q_copies, False, done)
    for_bottom(False, done)

    @pl.loop(0, rounds)
    def _(i):
        for_all(lambda k: copies(2 * i, k), False, done)


def per_device(nd, nl, displacement, velocity, inverse_mass, material, dilation_table, shear_table,
               stiffness_pair, impedance, bedrock_mask, incident):
    _, nz, ny, nx = displacement.shape
    steps = incident.shape[0]
    rounds = steps // 2
    nmat = dilation_table.shape[0]
    vmem = pl.BlockSpec(memory_space=pltpu.VMEM)
    hbm = pl.BlockSpec(memory_space=pltpu.MemorySpace.HBM)
    ext = nz + 4
    dma = pltpu.SemaphoreType.DMA
    return pl.pallas_call(
        functools.partial(kernel, nd, nl),
        out_shape=[jax.ShapeDtypeStruct(displacement.shape, f32)] * 2,
        in_specs=[hbm] * 10,
        out_specs=[vmem, vmem],
        scratch_shapes=[
            pltpu.VMEM((steps + 1, ext, 2, 3, ny, nx), f32),
            pltpu.VMEM((steps, ext, 3, ny, nx), f32),
            pltpu.VMEM((ext, 2, ny, nx), f32),
            pltpu.VMEM((ext, 2, ny, nx), f32),
            pltpu.VMEM((rounds, 2, 3, ny, nx), f32),
            pltpu.VMEM((rounds, ny, nx), f32),
            pltpu.VMEM((nz, ny, nx), i32),
            pltpu.VMEM(stiffness_pair.shape, f32),
            pltpu.VMEM((ny, nx), i32),
            pltpu.VMEM((steps, 3, ny, nx), f32),
            pltpu.VMEM((2, 48, KP), f32),
            pltpu.VMEM((MH, KP), bf16),
            pltpu.VMEM((ext, KL, nx), bf16),
            pltpu.VMEM((ext, KL, nx), bf16),
            pltpu.VMEM((2, MH, nx), f32),
            pltpu.VMEM((ext, 2, 2, ny, nx), f32),
            pltpu.VMEM((ext, 2, 2, ny, nx), f32),
            pltpu.VMEM((ext, ny, nx), f32),
            pltpu.SMEM((nmat,), f32),
            pltpu.SMEM((nmat,), f32),
            pltpu.SMEM((3,), f32),
            dma((14,)),
            dma((rounds, 16)),
            dma((rounds, 16)),
            dma((16,)),
            dma((16,)),
            dma((2,)),
            dma((2,)),
        ],
        compiler_params=pltpu.CompilerParams(
            collective_id=0, has_side_effects=True, vmem_limit_bytes=67043328),
    )(displacement, velocity, inverse_mass, material, dilation_table, shear_table,
      stiffness_pair, impedance, bedrock_mask, incident)


def solution(mesh):
    in_specs = (
        P(None, "depth", "lat", None),
        P(None, "depth", "lat", None),
        P("depth", "lat", None),
        P("depth", "lat", None),
        P(),
        P(),
        P(),
        P(),
        P("lat", None),
        P(None, None, "lat", None),
    )
    out_specs = (P(None, "depth", "lat", None), P(None, "depth", "lat", None))
    return jax.shard_map(
        functools.partial(per_device, mesh.shape["depth"], mesh.shape["lat"]),
        mesh=mesh, in_specs=in_specs, out_specs=out_specs, check_vma=False)
```

profile of v0, /device:TPU:47, one launch (start us, length us, event | category | flops | bytes accessed | tf_op | source)
XLA Modules:
  0.0 49.6 jit_solution(11619187989285795521)
XLA Ops:
  0.6 46.7 %shard_map.113 = (f32[3,8,8,256]{3,2,1,0:T(8,128)}, f32[3,8,8,256]{3,2,1,0:T(8,128)}) custom-call(f32[3,8,8,256]{3,2,1,0:T(8,128)} %u_in.1, f32[3,8,8,256]{3,2,1,0:T(8,128)} %v_in.1, f32[8,8,256]{2,1,0:T(8,128)} %im_in.1, s32[8,8,256]{2,1,0:T(8,128)} %mat_in.1, f32[8]{0:T(128)} %dil_in.1, f32[8]{0:T(128)} %she_in.1, f32[2,24,24]{2,1,0:T(8,128)} %k_in.1, ...), custom_call_target="tpu_custom_call" | custom-call | tf_op jit(solution)/shard_map/pallas_call | solution.py:364
  47.3 0.0 copy-start
  47.3 1.7 %copy.14 = f32[3,8,8,256]{3,2,1,0:T(8,128)} copy(f32[3,8,8,256]{3,2,1,0:T(8,128)} %get-tuple-element.4) | data formatting | bytes 393216
  49.0 0.0 copy-done
  49.0 0.7 %copy.15 = f32[3,8,8,256]{3,2,1,0:T(8,128)} copy(f32[3,8,8,256]{3,2,1,0:T(8,128)S(1)} %copy-done) | data formatting | bytes 393216
Async XLA Ops:
  47.3 1.7 %copy-start = (f32[3,8,8,256]{3,2,1,0:T(8,128)S(1)}, f32[3,8,8,256]{3,2,1,0:T(8,128)}, u32[]{:S(2)}) copy-start(f32[3,8,8,256]{3,2,1,0:T(8,128)} %get-tuple-element.5) | copy-start | bytes 589828
where the time goes:
time: 49.8 us; the launch traced here: 49.6 us
  Pallas kernels  46.7 us (94%)
  local copies, waits for them, and re-layouts  2.34 us (5%)
  between operations  0.65 us (1%)
    pallas_call x1, Pallas kernels, per_device(): pl.pallas_call(functools.partial(kernel, nd, nl), out_shape=[jax.ShapeDty...  46.7 us
    unnamed x4, local copies, waits for them, and re-layouts  2.34 us

commit v1 on v0

--- a/solution.py
+++ b/solution.py
@@ -36,6 +36,13 @@
     def exists(dz, dy):
         return ((d + dz >= 0) & (d + dz < nd)) & ((l + dy >= 0) & (l + dy < nl))
 
+    barrier = pltpu.get_barrier_semaphore()
+    partners = 0
+    for dz, dy in DIRECTIONS:
+        @pl.when(exists(dz, dy))
+        def _():
+            pl.semaphore_signal(barrier, inc=1, device_id=(d + dz, l + dy), device_id_type=MESH)
+        partners = partners + exists(dz, dy).astype(i32)
     own = pl.ds(2, nz)
     loads = [(im_in, Q.at[own, 0]), (mat_in, MI)]
     for c in range(3):
@@ -47,13 +54,6 @@
     for load in loads:
         load.start()
 
-    barrier = pltpu.get_barrier_semaphore()
-    partners = 0
-    for dz, dy in DIRECTIONS:
-        @pl.when(exists(dz, dy))
-        def _():
-            pl.semaphore_signal(barrier, inc=1, device_id=(d + dz, l + dy), device_id_type=MESH)
-        partners = partners + exists(dz, dy).astype(i32)
     for load in loads[:first]:
         load.wait()
     for z in range(nz):
@@ -70,38 +70,61 @@
             return own, own
         return (pl.ds(nz, 2), pl.ds(0, 2)) if dz == 1 else (pl.ds(2, 2), pl.ds(nz + 2, 2))
 
+    def rows_of(dy):
+        return (ny - 1, ny - 2, pl.ds(0, 3)) if dy == 1 else (0, 1, pl.ds(3, 3))
+
     def copies(t, k):
         dz, dy = DIRECTIONS[k]
         a, b = layers(dz)
         if dy == 0:
-            near, far = (nz + 1, nz) if dz == 1 else (2, 3)
-            to_near, to_far = (1, 0) if dz == 1 else (nz + 2, nz + 3)
-            pairs = [(W.at[t, near], W.at[t, to_near]), (W.at[t, far, 1], W.at[t, to_far, 1])]
+            pairs = [(W.at[t, a, 1], W.at[t, b, 1])]
         else:
-            rows, to = ((ny - 1, ny - 2), pl.ds(0, 3)) if dy == 1 else ((0, 1), pl.ds(3, 3))
-            pairs = [(W.at[t, a, :, :, rows[0]], HW.at[t, b, pl.ds(0, 2), to]),
-                     (W.at[t, a, 1, :, rows[1]], HW.at[t, b, 2, to])]
+            near_row, far_row, to = rows_of(dy)
+            pairs = [(W.at[t, a, 1, :, near_row], HW.at[t, b, 1, to]),
+                     (W.at[t, a, 1, :, far_row], HW.at[t, b, 2, to])]
         return [remote(src, dst, send_sem.at[t // 2, 2 * k + i], recv_sem.at[t // 2, 2 * k + i], dz, dy)
                 for i, (src, dst) in enumerate(pairs)]
 
-    def q_copies(k):
+    def first_copies(k):
         dz, dy = DIRECTIONS[k]
         a, b = layers(dz)
+        near, far = (nz + 1, nz) if dz == 1 else (2, 3)
+        to_near, to_far = (1, 0) if dz == 1 else (nz + 2, nz + 3)
         if dy == 0:
-            pairs = [(Q.at[a], Q.at[b])]
-        elif dy == 1:
-            pairs = [(Q.at[a, :, ny - 1], HQ.at[b, :, 0]), (Q.at[a, :, ny - 2], HQ.at[b, :, 1])]
+            pairs = [(W.at[0, near], W.at[0, to_near]), (W.at[0, far, 1], W.at[0, to_far, 1]),
+                     (Q.at[near], Q.at[to_near])]
+            if dz == 1:
+                pairs.append((Q.at[far, 1], Q.at[to_far, 1]))
         else:
-            pairs = [(Q.at[a, :, 0], HQ.at[b, :, 2])]
-        return [remote(src, dst, qsend_sem.at[2 * k + i], qrecv_sem.at[2 * k + i], dz, dy)
+            near_row, far_row, to = rows_of(dy)
+            slot = 0 if dy == 1 else 2
+            pairs = [(W.at[0, a, 1, :, far_row], HW.at[0, b, 2, to])]
+            if dz == 0:
+                pairs += [(W.at[0, a, :, :, near_row], HW.at[0, b, pl.ds(0, 2), to]),
+                          (Q.at[a, :, near_row], HQ.at[b, :, slot])]
+                if dy == 1:
+                    pairs.append((Q.at[a, 1, far_row], HQ.at[b, 1, 1]))
+            else:
+                pairs += [(W.at[0, near, :, :, near_row], HW.at[0, to_near, pl.ds(0, 2), to]),
+                          (W.at[0, far, 1, :, near_row], HW.at[0, to_far, 1, to]),
+                          (Q.at[near, :, near_row], HQ.at[to_near, :, slot])]
+                if dz == 1:
+                    pairs.append((Q.at[far, 1, near_row], HQ.at[to_far, 1, slot]))
+                if dy == 1:
+                    if dz == 1:
+                        pairs.append((Q.at[a, 1, far_row], HQ.at[b, 1, 1]))
+                    else:
+                        pairs.append((Q.at[near, 1, far_row], HQ.at[to_near, 1, 1]))
+        return [remote(src, dst, qsend_sem.at[6 * k + i], qrecv_sem.at[6 * k + i], dz, dy)
                 for i, (src, dst) in enumerate(pairs)]
 
     def b_copy(dy):
         row, to, i = (ny - 1, pl.ds(0, 3), 0) if dy == 1 else (0, pl.ds(3, 3), 1)
         return remote(BI.at[:, 0, :, row], HB.at[:, to], bsend_sem.at[i], brecv_sem.at[i], 0, dy)
 
-    def for_all(make, backward, act):
-        for k, (dz, dy) in enumerate(DIRECTIONS):
+    def for_all(make, backward, act, which=tuple(range(len(DIRECTIONS)))):
+        for k in which:
+            dz, dy = DIRECTIONS[k]
             sign = -1 if backward else 1
 
             @pl.when(exists(sign * dz, sign * dy))
@@ -116,7 +139,7 @@
                 act(b_copy(dy))
 
     start = lambda copy: copy.start()
-    for_all(lambda k: copies(0, k) + q_copies(k), False, start)
+    for_all(first_copies, False, start)
 
     for load in loads[first:]:
         load.wait()
@@ -154,6 +177,10 @@
             HQ[n, 1, q_rows[0]:q_rows[1]] = jnp.full((q_rows[1] - q_rows[0], nx), -1.0, f32)
         for r in range(rounds):
             HB[r, rows[0]:rows[1]] = jnp.zeros((3, nx), f32)
+
+    @pl.when(d < nd - 1)
+    def _():
+        HB[...] = jnp.zeros_like(HB)
 
     @pl.when(l == 0)
     def _():
@@ -241,10 +268,12 @@
         low, high = HQ[n, 0, 0:1], HQ[n, 0, 2:3]
         HIM[n] = DT * jnp.where(row < 3, jnp.broadcast_to(low, (ny, nx)), jnp.broadcast_to(high, (ny, nx)))
 
-    for_all(q_copies, True, lambda copy: copy.wait_recv())
-    for_bottom(True, lambda copy: copy.wait_recv())
-
-    @pl.loop(0, nz + 3)
+    here = lambda copy: copy.wait_recv()
+    lat_k, depth_k = (6, 7), (0, 1, 2, 3, 4, 5)
+    for_all(first_copies, True, here, lat_k)
+    for_bottom(True, here)
+
+    @pl.loop(2, nz + 2)
     def _(n):
         fields(n)
         masses(n)
@@ -273,57 +302,68 @@
         XH[n] = hi
         XL[n] = (x - hi.astype(f32)).astype(bf16)
 
-    def step(t, r, extended):
-        first_e, last_e = (0, nz + 3) if extended else (1, nz + 2)
+    def element(e, extended):
         m = MH if extended else MO
-        for n in range(first_e, last_e + 1):
-            operand(t, n, extended)
-        carry = None
-        for e in range(first_e, last_e):
-            x = jnp.concatenate([XH[e], XH[e + 1], XL[e], XL[e + 1], XH[e], XH[e + 1],
-                                 jnp.zeros((KP - 3 * KB, nx), bf16)], 0)
-            slot = e % 2
-            PR[slot, 0:m] = jnp.dot(WM[0:m], x, preferred_element_type=f32)
-
-            def gather(az):
-                sums = {}
-                for ax in (0, 1):
-                    for c in range(4 if extended else 3):
-                        total = None
-                        for f in (0, 1):
-                            for ay in (0, 1):
-                                g = 8 * f + 4 * az + 2 * ay + ax
-                                if c < 3:
-                                    at = 8 * (3 * g + c)
-                                    term = FD[e, f, ay] * PR[slot, at:at + 8]
-                                else:
-                                    at = MO + 8 * g
-                                    term = FH[e, f, ay] * PR[slot, at:at + 8]
-                                total = term if total is None else total + term
-                        sums[ax, c] = total
-                return sums
-
-            if carry is not None:
-                sums = gather(0)
-                force = [sums[0, c] + carry[0, c] + behind(sums[1, c] + carry[1, c])
-                         for c in range(4 if extended else 3)]
-                scale = DT * Q[e, 0]
-                for c in range(3):
-                    net = -force[c]
-                    v = W[t, e, 0, c]
-                    if e == nz + 1:
-                        net = net + at_bottom * imp[c] * (BI[t // 2, r, c] - v)
-                    v = v + scale * net
-                    W[t + 1, e, 0, c] = v
-                    W[t + 1, e, 1, c] = W[t, e, 1, c] + DT * v
-                if extended:
-                    net = -force[3]
-                    v = HW[t, e, 0]
-                    if e == nz + 1:
-                        net = net + at_bottom * imp_rows * (HB[t // 2] - v)
-                    v = v + HIM[e] * net
-                    HW[t + 1, e, 1] = HW[t, e, 1] + DT * v
-            carry = gather(1)
+        x = jnp.concatenate([XH[e], XH[e + 1], XL[e], XL[e + 1], XH[e], XH[e + 1],
+                             jnp.zeros((KP - 3 * KB, nx), bf16)], 0)
+        slot = e % 2
+        PR[slot, 0:m] = jnp.dot(WM[0:m], x, preferred_element_type=f32)
+        sides = []
+        for az in (0, 1):
+            sums = {}
+            for ax in (0, 1):
+                for c in range(4 if extended else 3):
+                    total = None
+                    for f in (0, 1):
+                        for ay in (0, 1):
+                            g = 8 * f + 4 * az + 2 * ay + ax
+                            if c < 3:
+                                at = 8 * (3 * g + c)
+                                term = FD[e, f, ay] * PR[slot, at:at + 8]
+                            else:
+                                at = MO + 8 * g
+                                term = FH[e, f, ay] * PR[slot, at:at + 8]
+                            total = term if total is None else total + term
+                    sums[ax, c] = total
+            sides.append(sums)
+        return sides
+
+    def advance(t, r, n, before, after, extended):
+        force = [after[0, c] + before[0, c] + behind(after[1, c] + before[1, c])
+                 for c in range(4 if extended else 3)]
+        scale = DT * Q[n, 0]
+        for c in range(3):
+            net = -force[c]
+            v = W[t, n, 0, c]
+            if n == nz + 1:
+                net = net + at_bottom * imp[c] * (BI[t // 2, r, c] - v)
+            v = v + scale * net
+            W[t + 1, n, 0, c] = v
+            W[t + 1, n, 1, c] = W[t, n, 1, c] + DT * v
+        if extended:
+            net = -force[3]
+            v = HW[t, n, 0]
+            if n == nz + 1:
+                net = net + at_bottom * imp_rows * (HB[t // 2] - v)
+            v = v + HIM[n] * net
+            HW[t + 1, n, 1] = HW[t, n, 1] + DT * v
+
+    def run(t, r, extended, order, nodes, low, high):
+        for e in order:
+            low[e], high[e] = element(e, extended)
+            for n in (e, e + 1):
+                if n in nodes and n in low and n - 1 in high:
+                    advance(t, r, n, high[n - 1], low[n], extended)
+                    nodes.remove(n)
+
+    def follow_tile(t, n):
+        HW[t, n, 0] = (HW[t, n, 1] - HW[t - 1, n, 1]) * (1.0 / DT)
+
+    def follow_layer(t, n):
+        for c in range(3):
+            W[t, n, 0, c] = (W[t, n, 1, c] - W[t - 1, n, 1, c]) * (1.0 / DT)
+
+    top = nz + 2
 
     @pl.loop(0, rounds)
     def _(i):
@@ -331,11 +371,52 @@
 
         @pl.when(i > 0)
         def _():
-            for_all(lambda k: copies(t, k), False, start)
-
-        for_all(lambda k: copies(t, k), True, lambda copy: copy.wait_recv())
-        step(t, 0, True)
-        step(t + 1, 1, False)
+            for_all(lambda k: copies(t, k), True, here, lat_k)
+            for n in range(2, top):
+                follow_tile(t, n)
+
+        low, high, nodes = {}, {}, set(range(1, top + 1))
+        for n in range(2, top):
+            operand(t, n, True)
+        run(t, 0, True, range(2, top - 1), nodes, low, high)
+
+        @pl.when(i == 0)
+        def _():
+            for_all(first_copies, True, here, depth_k)
+            for n in (0, 1, top):
+                fields(n)
+            for n in (1, top):
+                masses(n)
+
+        @pl.when(i > 0)
+        def _():
+            for_all(lambda k: copies(t, k), True, here, depth_k)
+            for n in (1, top):
+                follow_tile(t, n)
+                follow_layer(t, n)
+
+        for n in (1, 0, top, top + 1):
+            operand(t, n, True)
+        run(t, 0, True, (1, 0, top - 1, top), nodes, low, high)
+
+        def send(which):
+            @pl.when(i < rounds - 1)
+            def _():
+                for_all(lambda k: copies(t + 2, k), False, start, which)
+
+        low, high, nodes = {}, {}, set(range(2, top))
+        for n in range(1, 5):
+            operand(t + 1, n, False)
+        run(t + 1, 1, False, (1, 2, 3), nodes, low, high)
+        send((1, 4, 5))
+        for n in range(top - 3, top + 1):
+            operand(t + 1, n, False)
+        run(t + 1, 1, False, (top - 3, top - 2, top - 1), nodes, low, high)
+        send((0, 2, 3))
+        for n in range(5, top - 3):
+            operand(t + 1, n, False)
+        run(t + 1, 1, False, range(4, top - 3), nodes, low, high)
+        send(lat_k)
 
     for z in range(nz):
         for c in range(3):
@@ -343,10 +424,10 @@
             v_out[c, z] = W[steps, z + 2, 0, c]
 
     done = lambda copy: copy.wait_send()
-    for_all(q_copies, False, done)
+    for_all(first_copies, False, done)
     for_bottom(False, done)
 
-    @pl.loop(0, rounds)
+    @pl.loop(1, rounds)
     def _(i):
         for_all(lambda k: copies(2 * i, k), False, done)
 
@@ -391,15 +472,16 @@
             dma((14,)),
             dma((rounds, 16)),
             dma((rounds, 16)),
-            dma((16,)),
-            dma((16,)),
+            dma((48,)),
+            dma((48,)),
             dma((2,)),
             dma((2,)),
         ],
         compiler_params=pltpu.CompilerParams(
-            collective_id=0, has_side_effects=True, vmem_limit_bytes=67043328),
-    )(displacement, velocity, inverse_mass, material, dilation_table, shear_table,
-      stiffness_pair, impedance, bedrock_mask, incident)
+            collective_id=0, has_side_effects=True, vmem_limit_bytes=48 * 1024 * 1024),
+    )(*(pltpu.with_memory_space_constraint(x, pltpu.MemorySpace.HBM) for x in (
+        displacement, velocity, inverse_mass, material, dilation_table, shear_table,
+        stiffness_pair, impedance, bedrock_mask, incident)))
 
 
 def solution(mesh):

time: 49.8 us -> 44.3 us (0.89)
  the two profiles are of different devices: /device:TPU:47 before, /device:TPU:23 now
where the time goes in v1:
time: 44.3 us; the launch traced here: 44.2 us
  Pallas kernels  42.2 us (95%)
  local copies, waits for them, and re-layouts  1.36 us (3%)
  between operations  0.64 us (1%)
    pallas_call x1, Pallas kernels, per_device(): pl.pallas_call(functools.partial(kernel, nd, nl), out_shape=[jax.ShapeDty...  42.2 us
    unnamed x2, local copies, waits for them, and re-layouts  1.36 us

profile of v1, /device:TPU:23, one launch (start us, length us, event | category | flops | bytes accessed | tf_op | source)
XLA Modules:
  0.0 44.2 jit_solution(16772114062482524214)
XLA Ops:
  0.6 42.2 %shard_map.113 = (f32[3,8,8,256]{3,2,1,0:T(8,128)S(1)}, f32[3,8,8,256]{3,2,1,0:T(8,128)S(1)}) custom-call(f32[3,8,8,256]{3,2,1,0:T(8,128)} %u_in.1, f32[3,8,8,256]{3,2,1,0:T(8,128)} %v_in.1, f32[8,8,256]{2,1,0:T(8,128)} %im_in.1, s32[8,8,256]{2,1,0:T(8,128)} %mat_in.1, f32[8]{0:T(128)} %dil_in.1, f32[8]{0:T(128)} %she_in.1, f32[2,24,24]{2,1,0:T(8,128)} %k_in.1, ...), custom_call_target="tpu_custom_call" | custom-call | tf_op jit(solution)/shard_map/pallas_call | solution.py:445
  42.9 0.7 %copy.14 = f32[3,8,8,256]{3,2,1,0:T(8,128)} copy(f32[3,8,8,256]{3,2,1,0:T(8,128)S(1)} %get-tuple-element.4) | data formatting | bytes 393216
  43.5 0.7 %copy.15 = f32[3,8,8,256]{3,2,1,0:T(8,128)} copy(f32[3,8,8,256]{3,2,1,0:T(8,128)S(1)} %get-tuple-element.5) | data formatting | bytes 393216

commit v2 on v1

--- a/solution.py
+++ b/solution.py
@@ -269,7 +269,7 @@
         HIM[n] = DT * jnp.where(row < 3, jnp.broadcast_to(low, (ny, nx)), jnp.broadcast_to(high, (ny, nx)))
 
     here = lambda copy: copy.wait_recv()
-    lat_k, depth_k = (6, 7), (0, 1, 2, 3, 4, 5)
+    lat_k = (6, 7)
     for_all(first_copies, True, here, lat_k)
     for_bottom(True, here)
 
@@ -380,43 +380,63 @@
             operand(t, n, True)
         run(t, 0, True, range(2, top - 1), nodes, low, high)
 
-        @pl.when(i == 0)
-        def _():
-            for_all(first_copies, True, here, depth_k)
-            for n in (0, 1, top):
-                fields(n)
-            for n in (1, top):
-                masses(n)
-
-        @pl.when(i > 0)
-        def _():
-            for_all(lambda k: copies(t, k), True, here, depth_k)
-            for n in (1, top):
-                follow_tile(t, n)
-                follow_layer(t, n)
-
-        for n in (1, 0, top, top + 1):
-            operand(t, n, True)
-        run(t, 0, True, (1, 0, top - 1, top), nodes, low, high)
+        sides = {
+            "low": ((0, 2, 3), (1, 0), 1, (1, 0)),
+            "high": ((1, 4, 5), (top, top + 1), top, (top - 1, top)),
+        }
+
+        def finish_side(name, low, high, nodes):
+            which, layers_in, edge, order = sides[name]
+
+            @pl.when(i == 0)
+            def _():
+                for_all(first_copies, True, here, which)
+                for n in (0, 1) if name == "low" else (top,):
+                    fields(n)
+                masses(edge)
+
+            @pl.when(i > 0)
+            def _():
+                for_all(lambda k: copies(t, k), True, here, which)
+                follow_tile(t, edge)
+                follow_layer(t, edge)
+
+            for n in layers_in:
+                operand(t, n, True)
+            run(t, 0, True, order, nodes, low, high)
 
         def send(which):
             @pl.when(i < rounds - 1)
             def _():
                 for_all(lambda k: copies(t + 2, k), False, start, which)
 
-        low, high, nodes = {}, {}, set(range(2, top))
-        for n in range(1, 5):
-            operand(t + 1, n, False)
-        run(t + 1, 1, False, (1, 2, 3), nodes, low, high)
-        send((1, 4, 5))
-        for n in range(top - 3, top + 1):
-            operand(t + 1, n, False)
-        run(t + 1, 1, False, (top - 3, top - 2, top - 1), nodes, low, high)
-        send((0, 2, 3))
-        for n in range(5, top - 3):
-            operand(t + 1, n, False)
-        run(t + 1, 1, False, range(4, top - 3), nodes, low, high)
-        send(lat_k)
+        def rest(names):
+            low_a, high_a, nodes_a = dict(low), dict(high), set(nodes)
+            for name in names:
+                finish_side(name, low_a, high_a, nodes_a)
+            low_b, high_b, nodes_b = {}, {}, set(range(2, top))
+            done = set()
+            for name in names[::-1]:
+                order = (1, 2, 3) if name == "low" else (top - 3, top - 2, top - 1)
+                for n in range(order[0], order[-1] + 2):
+                    if n not in done:
+                        operand(t + 1, n, False)
+                        done.add(n)
+                run(t + 1, 1, False, order, nodes_b, low_b, high_b)
+                send((1, 4, 5) if name == "low" else (0, 2, 3))
+            for n in range(1, top + 1):
+                if n not in done:
+                    operand(t + 1, n, False)
+            run(t + 1, 1, False, range(4, top - 3), nodes_b, low_b, high_b)
+            send(lat_k)
+
+        @pl.when(d < nd // 2)
+        def _():
+            rest(("low", "high"))
+
+        @pl.when(d >= nd // 2)
+        def _():
+            rest(("high", "low"))
 
     for z in range(nz):
         for c in range(3):
@@ -430,6 +450,15 @@
     @pl.loop(1, rounds)
     def _(i):
         for_all(lambda k: copies(2 * i, k), False, done)
+
+
+def put_out(u, v, u_hbm, v_hbm, sem):
+    copies = [pltpu.make_async_copy(a.at[c], b.at[c], sem.at[3 * i + c])
+              for i, (a, b) in enumerate(((u, u_hbm), (v, v_hbm))) for c in range(3)]
+    for copy in copies:
+        copy.start()
+    for copy in copies:
+        copy.wait()
 
 
 def per_device(nd, nl, displacement, velocity, inverse_mass, material, dilation_table, shear_table,
@@ -442,7 +471,7 @@
     hbm = pl.BlockSpec(memory_space=pltpu.MemorySpace.HBM)
     ext = nz + 4
     dma = pltpu.SemaphoreType.DMA
-    return pl.pallas_call(
+    state = pl.pallas_call(
         functools.partial(kernel, nd, nl),
         out_shape=[jax.ShapeDtypeStruct(displacement.shape, f32)] * 2,
         in_specs=[hbm] * 10,
@@ -482,6 +511,14 @@
     )(*(pltpu.with_memory_space_constraint(x, pltpu.MemorySpace.HBM) for x in (
         displacement, velocity, inverse_mass, material, dilation_table, shear_table,
         stiffness_pair, impedance, bedrock_mask, incident)))
+    return pl.pallas_call(
+        put_out,
+        out_shape=[jax.ShapeDtypeStruct(displacement.shape, f32)] * 2,
+        in_specs=[vmem, vmem],
+        out_specs=[pl.BlockSpec(memory_space=pltpu.MemorySpace.HBM)] * 2,
+        scratch_shapes=[dma((6,))],
+        compiler_params=pltpu.CompilerParams(vmem_limit_bytes=2 * 1024 * 1024),
+    )(*state)
 
 
 def solution(mesh):

time: 44.3 us -> 43.7 us (0.986)
  local copies, waits for them, and re-layouts: 1.36 us -> 0 us
  Pallas kernels: 42.2 us -> 42.9 us
    unnamed x2 -> x0, local copies, waits for them, and re-layouts: 1.36 us -> none
    pallas_call x0 -> x1, Pallas kernels: none -> 0.79 us  [per_device(): pl.pallas_call(put_out, out_shape=[jax.ShapeDtypeStruct(displacement.shap...]
where the time goes in v2:
time: 43.7 us; the launch traced here: 43.6 us
  Pallas kernels  42.9 us (98%)
  between operations  0.64 us (1%)
    pallas_call x1, Pallas kernels, per_device(): pl.pallas_call(functools.partial(kernel, nd, nl), out_shape=[jax.ShapeDty...  42.2 us

profile of v2, /device:TPU:23, one launch (start us, length us, event | category | flops | bytes accessed | tf_op | source)
XLA Modules:
  0.0 43.6 jit_solution(1274531872031389549)
XLA Ops:
  0.6 42.2 %shard_map.113 = (f32[3,8,8,256]{3,2,1,0:T(8,128)S(1)}, f32[3,8,8,256]{3,2,1,0:T(8,128)S(1)}) custom-call(f32[3,8,8,256]{3,2,1,0:T(8,128)} %u_in.1, f32[3,8,8,256]{3,2,1,0:T(8,128)} %v_in.1, f32[8,8,256]{2,1,0:T(8,128)} %im_in.1, s32[8,8,256]{2,1,0:T(8,128)} %mat_in.1, f32[8]{0:T(128)} %dil_in.1, f32[8]{0:T(128)} %she_in.1, f32[2,24,24]{2,1,0:T(8,128)} %k_in.1, ...), custom_call_target="tpu_custom_call" | custom-call | tf_op jit(solution)/shard_map/pallas_call | solution.py:474
  42.8 0.8 %shard_map.114 = (f32[3,8,8,256]{3,2,1,0:T(8,128)}, f32[3,8,8,256]{3,2,1,0:T(8,128)}) custom-call(f32[3,8,8,256]{3,2,1,0:T(8,128)S(1)} %get-tuple-element.4.u, f32[3,8,8,256]{3,2,1,0:T(8,128)S(1)} %get-tuple-element.5.v), custom_call_target="tpu_custom_call" | custom-call | tf_op jit(solution)/shard_map/pallas_call | solution.py:514

commit v3 on v2

--- a/solution.py
+++ b/solution.py
@@ -139,7 +139,7 @@
                 act(b_copy(dy))
 
     start = lambda copy: copy.start()
-    for_all(first_copies, False, start)
+    for_all(first_copies, False, start, (6,7,0,1,2,3,4,5))
 
     for load in loads[first:]:
         load.wait()

time: 43.7 us -> 42.7 us (0.977)
  Pallas kernels: 42.9 us -> 41.5 us
    pallas_call x1, Pallas kernels: 42.2 us -> 40.8 us  [per_device(): pl.pallas_call(functools.partial(kernel, nd, nl), out_shape=[jax.ShapeDty...]
where the time goes in v3:
time: 42.7 us; the launch traced here: 42.2 us
  Pallas kernels  41.5 us (97%)
  between operations  0.64 us (1%)
    pallas_call x1, Pallas kernels, per_device(): pl.pallas_call(functools.partial(kernel, nd, nl), out_shape=[jax.ShapeDty...  40.8 us

profile of v3, /device:TPU:23, one launch (start us, length us, event | category | flops | bytes accessed | tf_op | source)
XLA Modules:
  0.0 42.2 jit_solution(10008212439496849497)
XLA Ops:
  0.6 40.8 %shard_map.113 = (f32[3,8,8,256]{3,2,1,0:T(8,128)S(1)}, f32[3,8,8,256]{3,2,1,0:T(8,128)S(1)}) custom-call(f32[3,8,8,256]{3,2,1,0:T(8,128)} %u_in.1, f32[3,8,8,256]{3,2,1,0:T(8,128)} %v_in.1, f32[8,8,256]{2,1,0:T(8,128)} %im_in.1, s32[8,8,256]{2,1,0:T(8,128)} %mat_in.1, f32[8]{0:T(128)} %dil_in.1, f32[8]{0:T(128)} %she_in.1, f32[2,24,24]{2,1,0:T(8,128)} %k_in.1, ...), custom_call_target="tpu_custom_call" | custom-call | tf_op jit(solution)/shard_map/pallas_call | solution.py:474
  41.4 0.8 %shard_map.114 = (f32[3,8,8,256]{3,2,1,0:T(8,128)}, f32[3,8,8,256]{3,2,1,0:T(8,128)}) custom-call(f32[3,8,8,256]{3,2,1,0:T(8,128)S(1)} %get-tuple-element.4.u, f32[3,8,8,256]{3,2,1,0:T(8,128)S(1)} %get-tuple-element.5.v), custom_call_target="tpu_custom_call" | custom-call | tf_op jit(solution)/shard_map/pallas_call | solution.py:514

commit v4 on v3

--- a/solution.py
+++ b/solution.py
@@ -85,37 +85,30 @@
         return [remote(src, dst, send_sem.at[t // 2, 2 * k + i], recv_sem.at[t // 2, 2 * k + i], dz, dy)
                 for i, (src, dst) in enumerate(pairs)]
 
-    def first_copies(k):
+    def first_copies(k, part="all"):
         dz, dy = DIRECTIONS[k]
         a, b = layers(dz)
         near, far = (nz + 1, nz) if dz == 1 else (2, 3)
         to_near, to_far = (1, 0) if dz == 1 else (nz + 2, nz + 3)
         if dy == 0:
-            pairs = [(W.at[0, near], W.at[0, to_near]), (W.at[0, far, 1], W.at[0, to_far, 1]),
-                     (Q.at[near], Q.at[to_near])]
-            if dz == 1:
-                pairs.append((Q.at[far, 1], Q.at[to_far, 1]))
+            pairs = [(W.at[0, a, 1], W.at[0, b, 1])]
+            pairs.append((Q.at[a, 1], Q.at[b, 1]) if dz == 1 else (Q.at[near, 1], Q.at[to_near, 1]))
+            late = [(W.at[0, near, 0], W.at[0, to_near, 0]), (Q.at[near, 0], Q.at[to_near, 0])]
         else:
             near_row, far_row, to = rows_of(dy)
             slot = 0 if dy == 1 else 2
-            pairs = [(W.at[0, a, 1, :, far_row], HW.at[0, b, 2, to])]
-            if dz == 0:
-                pairs += [(W.at[0, a, :, :, near_row], HW.at[0, b, pl.ds(0, 2), to]),
-                          (Q.at[a, :, near_row], HQ.at[b, :, slot])]
-                if dy == 1:
-                    pairs.append((Q.at[a, 1, far_row], HQ.at[b, 1, 1]))
-            else:
-                pairs += [(W.at[0, near, :, :, near_row], HW.at[0, to_near, pl.ds(0, 2), to]),
-                          (W.at[0, far, 1, :, near_row], HW.at[0, to_far, 1, to]),
-                          (Q.at[near, :, near_row], HQ.at[to_near, :, slot])]
-                if dz == 1:
-                    pairs.append((Q.at[far, 1, near_row], HQ.at[to_far, 1, slot]))
-                if dy == 1:
-                    if dz == 1:
-                        pairs.append((Q.at[a, 1, far_row], HQ.at[b, 1, 1]))
-                    else:
-                        pairs.append((Q.at[near, 1, far_row], HQ.at[to_near, 1, 1]))
-        return [remote(src, dst, qsend_sem.at[6 * k + i], qrecv_sem.at[6 * k + i], dz, dy)
+            pairs = [(W.at[0, a, 1, :, near_row], HW.at[0, b, 1, to]),
+                     (W.at[0, a, 1, :, far_row], HW.at[0, b, 2, to])]
+            m, to_m = (near, to_near) if dz == -1 else (a, b)
+            pairs.append((Q.at[m, 1, near_row], HQ.at[to_m, 1, slot]))
+            if dy == 1:
+                pairs.append((Q.at[m, 1, far_row], HQ.at[to_m, 1, 1]))
+            n, to_n = (a, b) if dz == 0 else (near, to_near)
+            late = [(W.at[0, n, 0, :, near_row], HW.at[0, to_n, 0, to]),
+                    (Q.at[n, 0, near_row], HQ.at[to_n, 0, slot])]
+        offset = len(pairs) if part == "late" else 0
+        pairs = {"all": pairs + late, "early": pairs, "late": late}[part]
+        return [remote(src, dst, qsend_sem.at[6 * k + offset + i], qrecv_sem.at[6 * k + offset + i], dz, dy)
                 for i, (src, dst) in enumerate(pairs)]
 
     def b_copy(dy):
@@ -139,7 +132,9 @@
                 act(b_copy(dy))
 
     start = lambda copy: copy.start()
-    for_all(first_copies, False, start, (6,7,0,1,2,3,4,5))
+    for_all(first_copies, False, start, (6, 7))
+    for part in ("early", "late"):
+        for_all(lambda k: first_copies(k, part), False, start, (0, 1, 2, 3, 4, 5))
 
     for load in loads[first:]:
         load.wait()
@@ -390,10 +385,9 @@
 
             @pl.when(i == 0)
             def _():
-                for_all(first_copies, True, here, which)
+                for_all(lambda k: first_copies(k, "early"), True, here, which)
                 for n in (0, 1) if name == "low" else (top,):
                     fields(n)
-                masses(edge)
 
             @pl.when(i > 0)
             def _():
@@ -403,7 +397,15 @@
 
             for n in layers_in:
                 operand(t, n, True)
+            nodes.remove(edge)
             run(t, 0, True, order, nodes, low, high)
+
+            @pl.when(i == 0)
+            def _():
+                for_all(lambda k: first_copies(k, "late"), True, here, which)
+                masses(edge)
+
+            advance(t, 0, edge, high[edge - 1], low[edge], True)
 
         def send(which):
             @pl.when(i < rounds - 1)
@@ -412,22 +414,17 @@
 
         def rest(names):
             low_a, high_a, nodes_a = dict(low), dict(high), set(nodes)
-            for name in names:
+            low_b, high_b, nodes_b = {}, {}, set(range(2, top))
+            up = names[0] == "low"
+            layers_b = range(1, top + 1) if up else range(top, 0, -1)
+            order = range(1, top) if up else range(top - 1, 0, -1)
+            parts = ((layers_b[:-2], order[:-2]), (layers_b[-2:], order[-2:]))
+            for name, (ns, es) in zip(names, parts):
                 finish_side(name, low_a, high_a, nodes_a)
-            low_b, high_b, nodes_b = {}, {}, set(range(2, top))
-            done = set()
-            for name in names[::-1]:
-                order = (1, 2, 3) if name == "low" else (top - 3, top - 2, top - 1)
-                for n in range(order[0], order[-1] + 2):
-                    if n not in done:
-                        operand(t + 1, n, False)
-                        done.add(n)
-                run(t + 1, 1, False, order, nodes_b, low_b, high_b)
+                for n in ns:
+                    operand(t + 1, n, False)
+                run(t + 1, 1, False, es, nodes_b, low_b, high_b)
                 send((1, 4, 5) if name == "low" else (0, 2, 3))
-            for n in range(1, top + 1):
-                if n not in done:
-                    operand(t + 1, n, False)
-            run(t + 1, 1, False, range(4, top - 3), nodes_b, low_b, high_b)
             send(lat_k)
 
         @pl.when(d < nd // 2)

time: 42.7 us -> 41.8 us (0.979); the launches traced: 42.2 us -> 41.7 us
    pallas_call x1, Pallas kernels: 40.8 us -> 40.3 us  [per_device(): pl.pallas_call(functools.partial(kernel, nd, nl), out_shape=[jax.ShapeDty...]
where the time goes in v4:
time: 41.8 us; the launch traced here: 41.7 us
  Pallas kernels  41.1 us (98%)
  between operations  0.64 us (2%)
    pallas_call x1, Pallas kernels, per_device(): pl.pallas_call(functools.partial(kernel, nd, nl), out_shape=[jax.ShapeDty...  40.3 us

profile of v4, /device:TPU:23, one launch (start us, length us, event | category | flops | bytes accessed | tf_op | source)
XLA Modules:
  0.0 41.7 jit_solution(3586911559448745203)
XLA Ops:
  0.6 40.3 %shard_map.113 = (f32[3,8,8,256]{3,2,1,0:T(8,128)S(1)}, f32[3,8,8,256]{3,2,1,0:T(8,128)S(1)}) custom-call(f32[3,8,8,256]{3,2,1,0:T(8,128)} %u_in.1, f32[3,8,8,256]{3,2,1,0:T(8,128)} %v_in.1, f32[8,8,256]{2,1,0:T(8,128)} %im_in.1, s32[8,8,256]{2,1,0:T(8,128)} %mat_in.1, f32[8]{0:T(128)} %dil_in.1, f32[8]{0:T(128)} %she_in.1, f32[2,24,24]{2,1,0:T(8,128)} %k_in.1, ...), custom_call_target="tpu_custom_call" | custom-call | tf_op jit(solution)/shard_map/pallas_call | solution.py:471
  40.9 0.8 %shard_map.114 = (f32[3,8,8,256]{3,2,1,0:T(8,128)}, f32[3,8,8,256]{3,2,1,0:T(8,128)}) custom-call(f32[3,8,8,256]{3,2,1,0:T(8,128)S(1)} %get-tuple-element.4.u, f32[3,8,8,256]{3,2,1,0:T(8,128)S(1)} %get-tuple-element.5.v), custom_call_target="tpu_custom_call" | custom-call | tf_op jit(solution)/shard_map/pallas_call | solution.py:511

commit v5 on v4

--- a/solution.py
+++ b/solution.py
@@ -73,16 +73,26 @@
     def rows_of(dy):
         return (ny - 1, ny - 2, pl.ds(0, 3)) if dy == 1 else (0, 1, pl.ds(3, 3))
 
-    def copies(t, k):
+    def copies(t, k, up, part="all"):
         dz, dy = DIRECTIONS[k]
         a, b = layers(dz)
+        sem = 4 * k
         if dy == 0:
             pairs = [(W.at[t, a, 1], W.at[t, b, 1])]
         else:
             near_row, far_row, to = rows_of(dy)
-            pairs = [(W.at[t, a, 1, :, near_row], HW.at[t, b, 1, to]),
-                     (W.at[t, a, 1, :, far_row], HW.at[t, b, 2, to])]
-        return [remote(src, dst, send_sem.at[t // 2, 2 * k + i], recv_sem.at[t // 2, 2 * k + i], dz, dy)
+            if dz == 0:
+                early, late = (pl.ds(2, 6), pl.ds(8, 2)) if up else (pl.ds(4, 6), pl.ds(2, 2))
+                spans = {"all": (early, late), "early": (early,), "late": (late,)}[part]
+                pairs = []
+                for span in spans:
+                    pairs += [(W.at[t, span, 1, :, near_row], HW.at[t, span, 1, to]),
+                              (W.at[t, span, 1, :, far_row], HW.at[t, span, 2, to])]
+                sem += 2 if part == "late" else 0
+            else:
+                pairs = [(W.at[t, a, 1, :, near_row], HW.at[t, b, 1, to]),
+                         (W.at[t, a, 1, :, far_row], HW.at[t, b, 2, to])]
+        return [remote(src, dst, send_sem.at[t // 2, sem + i], recv_sem.at[t // 2, sem + i], dz, dy)
                 for i, (src, dst) in enumerate(pairs)]
 
     def first_copies(k, part="all"):
@@ -364,23 +374,12 @@
     def _(i):
         t = 2 * i
 
-        @pl.when(i > 0)
-        def _():
-            for_all(lambda k: copies(t, k), True, here, lat_k)
-            for n in range(2, top):
-                follow_tile(t, n)
-
-        low, high, nodes = {}, {}, set(range(1, top + 1))
-        for n in range(2, top):
-            operand(t, n, True)
-        run(t, 0, True, range(2, top - 1), nodes, low, high)
-
         sides = {
             "low": ((0, 2, 3), (1, 0), 1, (1, 0)),
             "high": ((1, 4, 5), (top, top + 1), top, (top - 1, top)),
         }
 
-        def finish_side(name, low, high, nodes):
+        def finish_side(name, up, low, high, nodes):
             which, layers_in, edge, order = sides[name]
 
             @pl.when(i == 0)
@@ -391,7 +390,7 @@
 
             @pl.when(i > 0)
             def _():
-                for_all(lambda k: copies(t, k), True, here, which)
+                for_all(lambda k: copies(t, k, up), True, here, which)
                 follow_tile(t, edge)
                 follow_layer(t, edge)
 
@@ -407,33 +406,62 @@
 
             advance(t, 0, edge, high[edge - 1], low[edge], True)
 
-        def send(which):
-            @pl.when(i < rounds - 1)
-            def _():
-                for_all(lambda k: copies(t + 2, k), False, start, which)
-
-        def rest(names):
-            low_a, high_a, nodes_a = dict(low), dict(high), set(nodes)
+        def work(up):
+            near, far = ("low", "high") if up else ("high", "low")
+            turn = (lambda x: list(x)) if up else (lambda x: list(x)[::-1])
+            own_layers = turn(range(2, top))
+            own_elements = turn(range(2, top - 1))
+            layers_b = turn(range(1, top + 1))
+            elements_b = turn(range(1, top))
+            low_a, high_a, nodes_a = {}, {}, set(range(1, top + 1))
             low_b, high_b, nodes_b = {}, {}, set(range(2, top))
-            up = names[0] == "low"
-            layers_b = range(1, top + 1) if up else range(top, 0, -1)
-            order = range(1, top) if up else range(top - 1, 0, -1)
-            parts = ((layers_b[:-2], order[:-2]), (layers_b[-2:], order[-2:]))
-            for name, (ns, es) in zip(names, parts):
-                finish_side(name, low_a, high_a, nodes_a)
+
+            def send(which, part="all"):
+                @pl.when(i < rounds - 1)
+                def _():
+                    for_all(lambda k: copies(t + 2, k, up, part), False, start, which)
+
+            def lat_rows(part, ns):
+                @pl.when(i > 0)
+                def _():
+                    for_all(lambda k: copies(t, k, up, part), True, here, lat_k)
+                    for n in ns:
+                        follow_tile(t, n)
+
+            def step_a(ns, es):
+                for n in ns:
+                    operand(t, n, True)
+                run(t, 0, True, es, nodes_a, low_a, high_a)
+
+            def step_b(ns, es):
                 for n in ns:
                     operand(t + 1, n, False)
                 run(t + 1, 1, False, es, nodes_b, low_b, high_b)
-                send((1, 4, 5) if name == "low" else (0, 2, 3))
-            send(lat_k)
+
+            def side_k(name):
+                return (1, 4, 5) if name == "low" else (0, 2, 3)
+
+            lat_rows("early", own_layers[:6])
+            step_a(own_layers[:6], own_elements[:5])
+            finish_side(near, up, low_a, high_a, nodes_a)
+            step_b(layers_b[:6], elements_b[:5])
+            send(side_k(near))
+            lat_rows("late", own_layers[6:])
+            step_a(own_layers[6:], own_elements[5:])
+            step_b(layers_b[6:8], elements_b[5:7])
+            send(lat_k, "early")
+            finish_side(far, up, low_a, high_a, nodes_a)
+            step_b(layers_b[8:], elements_b[7:])
+            send(side_k(far))
+            send(lat_k, "late")
 
         @pl.when(d < nd // 2)
         def _():
-            rest(("low", "high"))
+            work(True)
 
         @pl.when(d >= nd // 2)
         def _():
-            rest(("high", "low"))
+            work(False)
 
     for z in range(nz):
         for c in range(3):
@@ -446,7 +474,13 @@
 
     @pl.loop(1, rounds)
     def _(i):
-        for_all(lambda k: copies(2 * i, k), False, done)
+        @pl.when(d < nd // 2)
+        def _():
+            for_all(lambda k: copies(2 * i, k, True), False, done)
+
+        @pl.when(d >= nd // 2)
+        def _():
+            for_all(lambda k: copies(2 * i, k, False), False, done)
 
 
 def put_out(u, v, u_hbm, v_hbm, sem):
@@ -496,8 +530,8 @@
             pltpu.SMEM((nmat,), f32),
             pltpu.SMEM((3,), f32),
             dma((14,)),
-            dma((rounds, 16)),
-            dma((rounds, 16)),
+            dma((rounds, 32)),
+            dma((rounds, 32)),
             dma((48,)),
             dma((48,)),
             dma((2,)),

time: 41.8 us -> 40.8 us (0.976)
  the two profiles are of different devices: /device:TPU:23 before, /device:TPU:7 now
where the time goes in v5:
time: 40.8 us; the launch traced here: 40.7 us
  Pallas kernels  40 us (98%)
  between operations  0.64 us (2%)
    pallas_call x1, Pallas kernels, per_device(): pl.pallas_call(functools.partial(kernel, nd, nl), out_shape=[jax.ShapeDty...  39.2 us

profile of v5, /device:TPU:7, one launch (start us, length us, event | category | flops | bytes accessed | tf_op | source)
XLA Modules:
  0.0 40.7 jit_solution(15650520180496346139)
XLA Ops:
  0.6 39.2 %shard_map.113 = (f32[3,8,8,256]{3,2,1,0:T(8,128)S(1)}, f32[3,8,8,256]{3,2,1,0:T(8,128)S(1)}) custom-call(f32[3,8,8,256]{3,2,1,0:T(8,128)} %u_in.1, f32[3,8,8,256]{3,2,1,0:T(8,128)} %v_in.1, f32[8,8,256]{2,1,0:T(8,128)} %im_in.1, s32[8,8,256]{2,1,0:T(8,128)} %mat_in.1, f32[8]{0:T(128)} %dil_in.1, f32[8]{0:T(128)} %she_in.1, f32[2,24,24]{2,1,0:T(8,128)} %k_in.1, ...), custom_call_target="tpu_custom_call" | custom-call | tf_op jit(solution)/shard_map/pallas_call | solution.py:505
  39.9 0.8 %shard_map.114 = (f32[3,8,8,256]{3,2,1,0:T(8,128)}, f32[3,8,8,256]{3,2,1,0:T(8,128)}) custom-call(f32[3,8,8,256]{3,2,1,0:T(8,128)S(1)} %get-tuple-element.4.u, f32[3,8,8,256]{3,2,1,0:T(8,128)S(1)} %get-tuple-element.5.v), custom_call_target="tpu_custom_call" | custom-call | tf_op jit(solution)/shard_map/pallas_call | solution.py:545

commit v6 on v5

--- a/solution.py
+++ b/solution.py
@@ -15,8 +15,17 @@
 KL = 80
 KB = 2 * KL
 KP = 512
-MO = 384
 MH = 512
+
+
+def own_row(g):
+    f, az, rest = g // 8, (g // 4) % 2, g % 4
+    return (64, 256)[az] + 96 * f + 24 * rest
+
+
+def halo_row(g):
+    f, az, rest = g // 8, (g // 4) % 2, g % 4
+    return (0, 448)[az] + 32 * f + 8 * rest
 
 
 def kernel(
@@ -243,7 +252,9 @@
 
     for q in range(0, 48, 2):
         tiles = [band(r8, (p // 6) % 2, (wide(0, p), wide(1, p))) for p in (q, q + 1)]
-        WM[8 * q:8 * q + 16] = jnp.concatenate(tiles, 0).astype(bf16)
+        at = [own_row(p // 3) + 8 * (p % 3) for p in (q, q + 1)]
+        assert at[1] == at[0] + 8 and at[0] % 16 == 0
+        WM[at[0]:at[0] + 16] = jnp.concatenate(tiles, 0).astype(bf16)
     for g in range(0, 16, 2):
         tiles = []
         for p in (g, g + 1):
@@ -252,7 +263,7 @@
                 a, b, c = (wide(by, 3 * p + i) for i in range(3))
                 picks.append(jnp.where((r8 == 0) | (r8 == 3), a, jnp.where((r8 == 1) | (r8 == 4), b, c)))
             tiles.append(band(y_halo, (p // 2) % 2, picks))
-        WM[MO + 8 * g:MO + 8 * g + 16] = jnp.concatenate(tiles, 0).astype(bf16)
+        WM[halo_row(g):halo_row(g) + 16] = jnp.concatenate(tiles, 0).astype(bf16)
 
     def fields(n):
         def full(x):
@@ -307,14 +318,15 @@
         XH[n] = hi
         XL[n] = (x - hi.astype(f32)).astype(bf16)
 
-    def element(e, extended):
-        m = MH if extended else MO
+    def element(e, extended, which):
+        a = (0 if extended else 64) if 0 in which else 256
+        b = (MH if extended else 448) if 1 in which else 256
         x = jnp.concatenate([XH[e], XH[e + 1], XL[e], XL[e + 1], XH[e], XH[e + 1],
                              jnp.zeros((KP - 3 * KB, nx), bf16)], 0)
         slot = e % 2
-        PR[slot, 0:m] = jnp.dot(WM[0:m], x, preferred_element_type=f32)
-        sides = []
-        for az in (0, 1):
+        PR[slot, a:b] = jnp.dot(WM[a:b], x, preferred_element_type=f32)
+        sides = {}
+        for az in which:
             sums = {}
             for ax in (0, 1):
                 for c in range(4 if extended else 3):
@@ -323,14 +335,14 @@
                         for ay in (0, 1):
                             g = 8 * f + 4 * az + 2 * ay + ax
                             if c < 3:
-                                at = 8 * (3 * g + c)
+                                at = own_row(g) + 8 * c
                                 term = FD[e, f, ay] * PR[slot, at:at + 8]
                             else:
-                                at = MO + 8 * g
+                                at = halo_row(g)
                                 term = FH[e, f, ay] * PR[slot, at:at + 8]
                             total = term if total is None else total + term
                     sums[ax, c] = total
-            sides.append(sums)
+            sides[az] = sums
         return sides
 
     def advance(t, r, n, before, after, extended):
@@ -355,7 +367,13 @@
 
     def run(t, r, extended, order, nodes, low, high):
         for e in order:
-            low[e], high[e] = element(e, extended)
+            first_e, last_e = (0, nz + 2) if extended else (1, nz + 1)
+            which = (1,) if e == first_e else (0,) if e == last_e else (0, 1)
+            sides = element(e, extended, which)
+            if 0 in which:
+                low[e] = sides[0]
+            if 1 in which:
+                high[e] = sides[1]
             for n in (e, e + 1):
                 if n in nodes and n in low and n - 1 in high:
                     advance(t, r, n, high[n - 1], low[n], extended)
@@ -384,9 +402,10 @@
 
             @pl.when(i == 0)
             def _():
-                for_all(lambda k: first_copies(k, "early"), True, here, which)
+                for_all(first_copies, True, here, which)
                 for n in (0, 1) if name == "low" else (top,):
                     fields(n)
+                masses(edge)
 
             @pl.when(i > 0)
             def _():
@@ -396,15 +415,7 @@
 
             for n in layers_in:
                 operand(t, n, True)
-            nodes.remove(edge)
             run(t, 0, True, order, nodes, low, high)
-
-            @pl.when(i == 0)
-            def _():
-                for_all(lambda k: first_copies(k, "late"), True, here, which)
-                masses(edge)
-
-            advance(t, 0, edge, high[edge - 1], low[edge], True)
 
         def work(up):
             near, far = ("low", "high") if up else ("high", "low")

time: 40.8 us -> 39.8 us (0.975)
  the two profiles are of different devices: /device:TPU:7 before, /device:TPU:23 now
where the time goes in v6:
time: 39.8 us; the launch traced here: 39.6 us
  Pallas kernels  39 us (98%)
  between operations  0.64 us (2%)
    pallas_call x1, Pallas kernels, per_device(): pl.pallas_call(functools.partial(kernel, nd, nl), out_shape=[jax.ShapeDty...  38.2 us

profile of v6, /device:TPU:23, one launch (start us, length us, event | category | flops | bytes accessed | tf_op | source)
XLA Modules:
  0.0 39.6 jit_solution(11048145240016818714)
XLA Ops:
  0.6 38.2 %shard_map.113 = (f32[3,8,8,256]{3,2,1,0:T(8,128)S(1)}, f32[3,8,8,256]{3,2,1,0:T(8,128)S(1)}) custom-call(f32[3,8,8,256]{3,2,1,0:T(8,128)} %u_in.1, f32[3,8,8,256]{3,2,1,0:T(8,128)} %v_in.1, f32[8,8,256]{2,1,0:T(8,128)} %im_in.1, s32[8,8,256]{2,1,0:T(8,128)} %mat_in.1, f32[8]{0:T(128)} %dil_in.1, f32[8]{0:T(128)} %she_in.1, f32[2,24,24]{2,1,0:T(8,128)} %k_in.1, ...), custom_call_target="tpu_custom_call" | custom-call | tf_op jit(solution)/shard_map/pallas_call | solution.py:516
  38.8 0.8 %shard_map.114 = (f32[3,8,8,256]{3,2,1,0:T(8,128)}, f32[3,8,8,256]{3,2,1,0:T(8,128)}) custom-call(f32[3,8,8,256]{3,2,1,0:T(8,128)S(1)} %get-tuple-element.4.u, f32[3,8,8,256]{3,2,1,0:T(8,128)S(1)} %get-tuple-element.5.v), custom_call_target="tpu_custom_call" | custom-call | tf_op jit(solution)/shard_map/pallas_call | solution.py:556

commit v7 on v6

--- a/solution.py
+++ b/solution.py
@@ -152,8 +152,14 @@
 
     start = lambda copy: copy.start()
     for_all(first_copies, False, start, (6, 7))
-    for part in ("early", "late"):
-        for_all(lambda k: first_copies(k, part), False, start, (0, 1, 2, 3, 4, 5))
+
+    @pl.when(d < nd // 2)
+    def _():
+        for_all(first_copies, False, start, (0, 2, 3, 1, 4, 5))
+
+    @pl.when(d >= nd // 2)
+    def _():
+        for_all(first_copies, False, start, (1, 4, 5, 0, 2, 3))
 
     for load in loads[first:]:
         load.wait()
@@ -323,7 +329,7 @@
         b = (MH if extended else 448) if 1 in which else 256
         x = jnp.concatenate([XH[e], XH[e + 1], XL[e], XL[e + 1], XH[e], XH[e + 1],
                              jnp.zeros((KP - 3 * KB, nx), bf16)], 0)
-        slot = e % 2
+        slot = e % 4
         PR[slot, a:b] = jnp.dot(WM[a:b], x, preferred_element_type=f32)
         sides = {}
         for az in which:
@@ -533,7 +539,7 @@
             pltpu.VMEM((MH, KP), bf16),
             pltpu.VMEM((ext, KL, nx), bf16),
             pltpu.VMEM((ext, KL, nx), bf16),
-            pltpu.VMEM((2, MH, nx), f32),
+            pltpu.VMEM((4, MH, nx), f32),
             pltpu.VMEM((ext, 2, 2, ny, nx), f32),
             pltpu.VMEM((ext, 2, 2, ny, nx), f32),
             pltpu.VMEM((ext, ny, nx), f32),

time: 39.8 us -> 39.7 us (level)
  no operation moved by 1% of the time
where the time goes in v7:
time: 39.7 us; the launch traced here: 39.5 us
  Pallas kernels  38.9 us (98%)
  between operations  0.64 us (2%)
    pallas_call x1, Pallas kernels, per_device(): pl.pallas_call(functools.partial(kernel, nd, nl), out_shape=[jax.ShapeDty...  38.1 us

profile of v7, /device:TPU:23, one launch (start us, length us, event | category | flops | bytes accessed | tf_op | source)
XLA Modules:
  0.0 39.5 jit_solution(7682080220758807288)
XLA Ops:
  0.6 38.1 %shard_map.113 = (f32[3,8,8,256]{3,2,1,0:T(8,128)S(1)}, f32[3,8,8,256]{3,2,1,0:T(8,128)S(1)}) custom-call(f32[3,8,8,256]{3,2,1,0:T(8,128)} %u_in.1, f32[3,8,8,256]{3,2,1,0:T(8,128)} %v_in.1, f32[8,8,256]{2,1,0:T(8,128)} %im_in.1, s32[8,8,256]{2,1,0:T(8,128)} %mat_in.1, f32[8]{0:T(128)} %dil_in.1, f32[8]{0:T(128)} %she_in.1, f32[2,24,24]{2,1,0:T(8,128)} %k_in.1, ...), custom_call_target="tpu_custom_call" | custom-call | tf_op jit(solution)/shard_map/pallas_call | solution.py:522
  38.7 0.8 %shard_map.114 = (f32[3,8,8,256]{3,2,1,0:T(8,128)}, f32[3,8,8,256]{3,2,1,0:T(8,128)}) custom-call(f32[3,8,8,256]{3,2,1,0:T(8,128)S(1)} %get-tuple-element.4.u, f32[3,8,8,256]{3,2,1,0:T(8,128)S(1)} %get-tuple-element.5.v), custom_call_target="tpu_custom_call" | custom-call | tf_op jit(solution)/shard_map/pallas_call | solution.py:562

commit v8 on v7

--- a/solution.py
+++ b/solution.py
@@ -361,8 +361,12 @@
             if n == nz + 1:
                 net = net + at_bottom * imp[c] * (BI[t // 2, r, c] - v)
             v = v + scale * net
+            u = W[t, n, 1, c] + DT * v
             W[t + 1, n, 0, c] = v
-            W[t + 1, n, 1, c] = W[t, n, 1, c] + DT * v
+            W[t + 1, n, 1, c] = u
+            if not extended:
+                u_out[c, n - 2] = u
+                v_out[c, n - 2] = v
         if extended:
             net = -force[3]
             v = HW[t, n, 0]
@@ -479,11 +483,6 @@
         @pl.when(d >= nd // 2)
         def _():
             work(False)
-
-    for z in range(nz):
-        for c in range(3):
-            u_out[c, z] = W[steps, z + 2, 1, c]
-            v_out[c, z] = W[steps, z + 2, 0, c]
 
     done = lambda copy: copy.wait_send()
     for_all(first_copies, False, done)

time: 39.7 us -> 39.7 us (level)
  no operation moved by 1% of the time
where the time goes in v8:
time: 39.7 us; the launch traced here: 39.5 us
  Pallas kernels  38.9 us (98%)
  between operations  0.64 us (2%)
    pallas_call x1, Pallas kernels, per_device(): pl.pallas_call(functools.partial(kernel, nd, nl), out_shape=[jax.ShapeDty...  38.1 us

profile of v8, /device:TPU:23, one launch (start us, length us, event | category | flops | bytes accessed | tf_op | source)
XLA Modules:
  0.0 39.5 jit_solution(7945953954132537234)
XLA Ops:
  0.6 38.1 %shard_map.113 = (f32[3,8,8,256]{3,2,1,0:T(8,128)S(1)}, f32[3,8,8,256]{3,2,1,0:T(8,128)S(1)}) custom-call(f32[3,8,8,256]{3,2,1,0:T(8,128)} %u_in.1, f32[3,8,8,256]{3,2,1,0:T(8,128)} %v_in.1, f32[8,8,256]{2,1,0:T(8,128)} %im_in.1, s32[8,8,256]{2,1,0:T(8,128)} %mat_in.1, f32[8]{0:T(128)} %dil_in.1, f32[8]{0:T(128)} %she_in.1, f32[2,24,24]{2,1,0:T(8,128)} %k_in.1, ...), custom_call_target="tpu_custom_call" | custom-call | tf_op jit(solution)/shard_map/pallas_call | solution.py:521
  38.7 0.8 %shard_map.114 = (f32[3,8,8,256]{3,2,1,0:T(8,128)}, f32[3,8,8,256]{3,2,1,0:T(8,128)}) custom-call(f32[3,8,8,256]{3,2,1,0:T(8,128)S(1)} %get-tuple-element.4.u, f32[3,8,8,256]{3,2,1,0:T(8,128)S(1)} %get-tuple-element.5.v), custom_call_target="tpu_custom_call" | custom-call | tf_op jit(solution)/shard_map/pallas_call | solution.py:561
